TPU v7x, 32 devices: a whole 2x2x4 slice. The times are simulated.
32 devices in a mesh: groups: 2 (over y), expert: 4 (over z), tensor: 4 (over x, core).
Axes of the slice: x: 2, y: 2, z: 4, core: 2. Of those that a mesh axis runs over, the one named last changes fastest.
Arguments:
- tokens: bfloat16 [1024, 7168], P(('groups', 'expert'), 'tensor'), parts along dimension 0, may hold values from -6 to 6
- choices: int32 [1024, 4], P(('groups', 'expert')), parts along dimension 0, may hold values from 0 to 15, all different within a row; in each aligned block of 128 rows (0 to 127, 128 to 255, ...) at most 48 rows name the same one
- affinity: float32 [1024, 4], P(('groups', 'expert')), parts along dimension 0, may hold values from -6 to 6
- expert_gate: bfloat16 [7168, 16384], P('tensor', 'expert'), may hold values from -0.0625 to 0.0625
- expert_up: bfloat16 [7168, 16384], P('tensor', 'expert'), may hold values from -0.0625 to 0.0625
- expert_down: bfloat16 [16384, 7168], P('expert', 'tensor'), may hold values from -0.1875 to 0.1875
- shared_in: bfloat16 [2, 1024, 7168], P(None, 'expert', 'tensor'), may hold values from -0.0625 to 0.0625
- shared_down: bfloat16 [1024, 7168], P('expert', 'tensor'), may hold values from -0.1875 to 0.1875
Outputs:
- mixed: bfloat16 [1024, 7168], P(('groups', 'expert'), 'tensor'), parts along dimension 0
There are 2 independent parts, one for each index of `groups`. A program takes and returns all parts, laid end to end along the dimension named above; an argument that names none is the same for every part. Nothing has to cross between parts.
Inputs may be any that keep to these rules, and one draw needn't show every extreme that they name: `choices`: within the rows of one index of expert (128 tokens) every expert is named at most 48 times, a bound that some block reaches; a token names 4 different experts.
All inputs are finite; a program needn't handle non-finite values.
Results may differ from a plain program's by a relative error of at most 0.02.
Values may be sent and summed in bfloat16 or wider, within the bound.
A program may use at most 128 MiB of HBM per device.

v0:
```python
import functools

import jax
import jax.numpy as jnp
from jax import lax
from jax.experimental import pallas as pl
from jax.experimental.pallas import tpu as pltpu
from jax.sharding import PartitionSpec as P

FFE = 1024
CAP = 48
MESH = pl.DeviceIdType.MESH
F32 = jnp.float32
BF16 = jnp.bfloat16


def mm(a, b, ca=1, cb=0):
    return lax.dot_general(a, b, (((ca,), (cb,)), ((), ())), preferred_element_type=F32)


def ring_rows(tok, hops, hop, rightward):
    if hop < hops:
        return 0, tok
    return (0, tok // 2) if rightward else (tok // 2, tok // 2)


def layer(
    dims, tokens, meta, gate_hbm, up_hbm, down_hbm, sin_hbm, sdown_hbm, out,
    x_all, meta_all, gate_w, up_w, down_w, sin_w, sdown_w, rows_buf, comb,
    part, core_in, x_out, x_in, hid, s_part, s_core_in, s_x_out, s_x_in, s_hid,
    rs_out, rs_in,
    load_sem, gate_sem, up_sem, down_sem, meta_sem, ag_sem, core_sem, x_sem, hx_sem, hc_sem, rs_sem,
):
    ns, nx, local_count, piece, tok, cap, top = dims
    hops = ns // 2
    z, t = lax.axis_index("expert"), lax.axis_index("tensor")
    x, c = lax.div(t, 2), lax.rem(t, 2)
    peer_c = 1 - c
    peer_t = 2 * x + peer_c
    right, left = lax.rem(z + 1, ns), lax.rem(z + ns - 1, ns)
    slots = gate_w.shape[0]

    def zoff(k):
        return lax.rem(z + k + ns, ns)

    def remote(src, dst, sems, index, where):
        send = sems.at[(0,) + index]
        recv = sems.at[(1,) + index]
        return pltpu.make_async_remote_copy(
            src_ref=src, dst_ref=dst, send_sem=send, recv_sem=recv, device_id=where, device_id_type=MESH
        )

    own_tok = pltpu.make_async_copy(tokens, x_all.at[z], load_sem.at[0])
    own_meta = pltpu.make_async_copy(meta, meta_all.at[z], load_sem.at[1])
    own_tok.start()
    own_meta.start()
    barrier = pltpu.get_barrier_semaphore()
    for k in range(1, ns):
        pl.semaphore_signal(barrier, inc=1, device_id={"expert": zoff(k)}, device_id_type=MESH)
    for k in range(1, nx):
        pl.semaphore_signal(
            barrier, inc=1, device_id={"tensor": 2 * lax.rem(x + k, nx) + c}, device_id_type=MESH
        )
    pl.semaphore_signal(barrier, inc=1, device_id={"tensor": peer_t}, device_id_type=MESH)

    sin_load = pltpu.make_async_copy(sin_hbm, sin_w, load_sem.at[2])
    sdown_load = pltpu.make_async_copy(sdown_hbm, sdown_w, load_sem.at[3])
    sin_load.start()

    def cols(e):
        return pl.ds(e * piece, piece)

    gate_loads = [
        pltpu.make_async_copy(gate_hbm.at[:, cols(e)], gate_w.at[e % slots], gate_sem.at[e])
        for e in range(local_count)
    ]
    up_loads = [
        pltpu.make_async_copy(up_hbm.at[:, cols(e)], up_w.at[e % slots], up_sem.at[e])
        for e in range(local_count)
    ]
    down_loads = [
        pltpu.make_async_copy(down_hbm.at[cols(e), :], down_w.at[e], down_sem.at[e])
        for e in range(local_count)
    ]
    own_tok.wait()
    own_meta.wait()
    pl.semaphore_wait(barrier, (ns - 1) + (nx - 1) + 1)

    def ag_copy(hop, rightward):
        start, size = ring_rows(tok, hops, hop, rightward)
        block = zoff(1 - hop) if rightward else zoff(hop - 1)
        ref = x_all.at[block, pl.ds(start, size), :]
        where = {"expert": right if rightward else left}
        return remote(ref, ref, ag_sem, (0 if rightward else 1, hop - 1), where)

    ag = {(h, d): ag_copy(h, d) for h in range(1, hops + 1) for d in (True, False)}
    for d in (True, False):
        ag[1, d].start()
    meta_copies = []
    for k in range(1, ns):
        copy = remote(meta_all.at[z], meta_all.at[z], meta_sem, (k - 1,), {"expert": zoff(k)})
        copy.start()
        meta_copies.append(copy)
    for e in range(min(slots, local_count)):
        gate_loads[e].start()
        up_loads[e].start()
    for e in range(local_count):
        down_loads[e].start()
    sdown_load.start()

    tri = (
        lax.broadcasted_iota(jnp.int32, (tok, tok), 0) < lax.broadcasted_iota(jnp.int32, (tok, tok), 1)
    ).astype(F32).astype(BF16)
    slot_of = lax.broadcasted_iota(jnp.int32, (cap, tok), 0).astype(F32)
    mask_rows = -(-local_count // 8) * 8
    row_of = lax.broadcasted_iota(jnp.int32, (mask_rows, tok), 0)
    columns = local_count * piece

    def dispatch(s):
        info = meta_all[s]
        masks, weights = [], []
        mask_all = jnp.zeros((mask_rows, tok), F32)
        for l in range(local_count):
            eid = lax.div(z * columns + l * piece, FFE).astype(F32)
            hit = (info[:top] == eid).astype(F32)
            mask = jnp.sum(hit, axis=0, keepdims=True)
            masks.append(mask)
            weights.append(jnp.sum(hit * info[top : 2 * top], axis=0, keepdims=True))
            mask_all = jnp.where(row_of == l, mask, mask_all)
        position = mm(mask_all.astype(BF16), tri)
        picks = []
        for l in range(local_count):
            pick = jnp.where((slot_of == position[l : l + 1]) & (masks[l] > 0.5), 1.0, 0.0)
            picks.append(pick.astype(BF16))
            comb[s, pl.ds(l * cap, cap), :] = (pick * weights[l]).astype(BF16)
        stacked = jnp.concatenate(picks, axis=0) if local_count > 1 else picks[0]
        gathered = mm(stacked, x_all[s]).astype(BF16)
        for l in range(local_count):
            rows_buf[l, s] = gathered[l * cap : (l + 1) * cap]

    for copy in meta_copies:
        copy.wait()
    dispatch(z)
    for hop in range(1, hops + 1):
        for d in (True, False):
            ag[hop, d].wait()
            if hop < hops:
                ag[hop + 1, d].start()
        dispatch(zoff(-hop))
        if hop < hops:
            dispatch(zoff(hop))

    unit_count = local_count + 1

    def unit(u):
        if u == 0:
            return s_part, s_core_in, s_x_out, s_x_in, s_hid
        e = u - 1
        return part.at[e], core_in.at[e], x_out.at[e], x_in.at[e], hid.at[e]

    def first(u):
        p, ci, _, _, _ = unit(u)
        if u == 0:
            sin_load.wait()
            whole = x_all[...].reshape(ns * tok, x_all.shape[2])
            for g in range(2):
                p[g] = mm(whole, sin_w[g], 1, 1).astype(BF16)
        else:
            e = u - 1
            lhs = rows_buf[e].reshape(ns * cap, x_all.shape[2])
            gate_loads[e].wait()
            p[0] = mm(lhs, gate_w[e % slots]).astype(BF16)
            up_loads[e].wait()
            p[1] = mm(lhs, up_w[e % slots]).astype(BF16)
            if e + slots < local_count:
                gate_loads[e + slots].start()
                up_loads[e + slots].start()
        half = p.shape[1] // 2
        theirs = pl.ds(pl.multiple_of(peer_c * half, half), half)
        copy = remote(p.at[:, theirs, :], ci, core_sem, (u,), {"tensor": peer_t})
        copy.start()
        return copy

    def chunk(p, ci, which):
        half = p.shape[1] // 2
        q = half // nx
        mine = pl.ds(pl.multiple_of(c * half + which * q, q), q)
        there = pl.ds(pl.multiple_of(which * q, q), q)
        return [p[g, mine, :].astype(F32) + ci[g, there, :].astype(F32) for g in range(2)]

    def second(u, core_copy):
        p, ci, xo, xi, _ = unit(u)
        core_copy.wait()
        copies = []
        for k in range(1, nx):
            other = lax.rem(x + k, nx)
            sums = chunk(p, ci, other)
            for g in range(2):
                xo[k - 1, g] = sums[g].astype(BF16)
            copy = remote(xo.at[k - 1], xi.at[k - 1], x_sem, (u, k - 1), {"tensor": 2 * other + c})
            copy.start()
            copies.append(copy)
        return copies

    def hid_rows(h, which):
        half = h.shape[0] // 2
        q = half // nx
        return h.at[pl.ds(pl.multiple_of(c * half + which * q, q), q), :]

    def third(u, x_copies):
        p, ci, _, xi, h = unit(u)
        sums = chunk(p, ci, x)
        for k in range(1, nx):
            x_copies[k - 1].wait()
            for g in range(2):
                sums[g] = sums[g] + xi[k - 1, g].astype(F32)
        gate, up = sums
        value = (gate / (1.0 + jnp.exp(-gate)) * up).astype(BF16)
        ref = hid_rows(h, x)
        ref[...] = value
        x_sends = []
        for k in range(1, nx):
            where = {"tensor": 2 * lax.rem(x + k, nx) + c}
            copy = remote(ref, ref, hx_sem, (u, k - 1), where)
            copy.start()
            x_sends.append(copy)
        copy = remote(ref, ref, hc_sem, (u, 0), {"tensor": peer_t})
        copy.start()
        return x_sends, [copy]

    def fourth(u, x_sends, core_sends):
        h = unit(u)[4]
        for k in range(1, nx):
            x_sends[k - 1].wait()
            ref = hid_rows(h, lax.rem(x + nx - k, nx))
            copy = remote(ref, ref, hc_sem, (u, k), {"tensor": peer_t})
            copy.start()
            core_sends.append(copy)
        return core_sends

    def fifth(u, core_sends):
        for copy in core_sends:
            copy.wait()
        if u > 0:
            e = u - 1
            down_loads[e].wait()
            made = mm(hid[e], down_w[e]).astype(BF16)
            rows_buf[e] = made.reshape(ns, cap, made.shape[1])

    state = {}
    for u in range(unit_count + 1):
        if u < unit_count:
            state[u] = first(u)
        if u >= 1:
            state[u - 1] = second(u - 1, state[u - 1])
    for u in range(unit_count + 2):
        if u < unit_count:
            state[u] = third(u, state[u])
        if 1 <= u <= unit_count:
            state[u - 1] = fourth(u - 1, *state[u - 1])
        if u >= 2:
            fifth(u - 2, state[u - 2])

    sdown_load.wait()

    def partial(s):
        made = rows_buf[:, s].reshape(local_count * cap, x_all.shape[2])
        shared = s_hid[pl.ds(pl.multiple_of(s * tok, tok), tok), :]
        return mm(comb[s], made, 0, 0) + mm(shared, sdown_w[...])

    def rs_copy(hop, rightward):
        start, size = ring_rows(tok, hops, hop, rightward)
        d = 0 if rightward else 1
        span = pl.ds(start, size)
        where = {"expert": right if rightward else left}
        return remote(
            rs_out.at[d, hop - 1, span, :], rs_in.at[d, hop - 1, span, :], rs_sem, (d, hop - 1), where
        )

    def arrived(hop, rightward):
        start, size = ring_rows(tok, hops, hop, rightward)
        got = rs_in[0 if rightward else 1, hop - 1, pl.ds(start, size), :].astype(F32)
        if size == tok:
            return got
        fill = jnp.zeros((tok - size, got.shape[1]), F32)
        return jnp.concatenate([got, fill] if start == 0 else [fill, got], axis=0)

    rs = {(h, d): rs_copy(h, d) for h in range(1, hops + 1) for d in (True, False)}
    opposite = partial(zoff(hops)).astype(BF16)
    for d in (True, False):
        start, size = ring_rows(tok, hops, hops, d)
        rs_out[0 if d else 1, hops - 1, pl.ds(start, size), :] = opposite[start : start + size]
        rs[hops, d].start()
    for hop in range(hops - 1, 0, -1):
        for d in (True, False):
            value = partial(zoff(hop if d else -hop))
            rs[hop + 1, d].wait()
            rs_out[0 if d else 1, hop - 1] = (value + arrived(hop + 1, d)).astype(BF16)
            rs[hop, d].start()
    total = partial(z)
    for d in (True, False):
        rs[1, d].wait()
        total = total + arrived(1, d)
    out[...] = total.astype(BF16)


def line_layer(
    dims, tokens, meta, gate_hbm, up_hbm, down_hbm, sin_hbm, sdown_hbm, out,
    x_all, meta_all, gate_w, up_w, down_w, sin_w, sdown_w, rows, made, comb,
    part, core_in, x_out, x_in, hid, s_part, s_core_in, s_x_out, s_x_in, s_hid, rs_in,
    load_sem, gate_sem, up_sem, down_sem, meta_sem, ag_sem, core_sem, x_sem, hx_sem, hc_sem, rs_sem,
):
    ns, nx, local_count, piece, tok, cap, top, pieces, cw = dims
    width = x_all.shape[2]
    z, t = lax.axis_index("expert"), lax.axis_index("tensor")
    x, c = lax.div(t, 2), lax.rem(t, 2)
    peer_c = 1 - c
    peer_t = 2 * x + peer_c
    mir = lax.div(z, ns // 2)
    zeta = z + mir * (ns - 1 - 2 * z)
    above = z + 1 - 2 * mir
    below = z - 1 + 2 * mir
    spread = tok // pieces

    def phys(b):
        return b + mir * (ns - 1 - 2 * b)

    def zoff(k):
        return lax.rem(z + k + ns, ns)

    def remote(src, dst, sems, index, where):
        send = sems.at[(0,) + index]
        recv = sems.at[(1,) + index]
        return pltpu.make_async_remote_copy(
            src_ref=src, dst_ref=dst, send_sem=send, recv_sem=recv, device_id=where, device_id_type=MESH
        )

    own_tok = pltpu.make_async_copy(tokens, x_all.at[z], load_sem.at[0])
    own_meta = pltpu.make_async_copy(meta, meta_all.at[z], load_sem.at[1])
    own_tok.start()
    own_meta.start()
    barrier = pltpu.get_barrier_semaphore()
    for k in range(1, ns):
        pl.semaphore_signal(barrier, inc=1, device_id={"expert": zoff(k)}, device_id_type=MESH)
    for k in range(1, nx):
        pl.semaphore_signal(
            barrier, inc=1, device_id={"tensor": 2 * lax.rem(x + k, nx) + c}, device_id_type=MESH
        )
    pl.semaphore_signal(barrier, inc=1, device_id={"tensor": peer_t}, device_id_type=MESH)

    sin_load = pltpu.make_async_copy(sin_hbm, sin_w, load_sem.at[2])
    sdown_load = pltpu.make_async_copy(sdown_hbm, sdown_w, load_sem.at[3])

    def cols(e):
        return pl.ds(e * piece, piece)

    gate_loads = [
        pltpu.make_async_copy(gate_hbm.at[:, cols(e)], gate_w.at[e], gate_sem.at[e]) for e in range(local_count)
    ]
    up_loads = [
        pltpu.make_async_copy(up_hbm.at[:, cols(e)], up_w.at[e], up_sem.at[e]) for e in range(local_count)
    ]
    down_loads = [
        pltpu.make_async_copy(down_hbm.at[cols(e), :], down_w.at[e], down_sem.at[e]) for e in range(local_count)
    ]
    sin_load.start()
    for e in range(local_count):
        gate_loads[e].start()
        up_loads[e].start()
    for e in range(local_count):
        down_loads[e].start()
    sdown_load.start()
    own_tok.wait()
    own_meta.wait()
    pl.semaphore_wait(barrier, (ns - 1) + (nx - 1) + 1)

    def ag_copy(upward, b, k, where):
        d = mir if upward else 1 - mir
        block = phys(b)
        ref = x_all.at[block, pl.ds(k * spread, spread), :]
        return remote(ref, ref, ag_sem, (d, block, k), {"expert": where})

    for k in range(pieces):
        ag_copy(True, zeta, k, above).start()

        @pl.when(zeta > 0)
        def _():
            ag_copy(False, zeta, k, below).start()

    meta_copies = []
    for k in range(1, ns):
        copy = remote(meta_all.at[z], meta_all.at[z], meta_sem, (k - 1,), {"expert": zoff(k)})
        copy.start()
        meta_copies.append(copy)

    def from_above(b, k):
        ag_copy(False, b, k, above).wait_recv()

        @pl.when(zeta > 0)
        def _():
            ag_copy(False, b, k, below).start()

    def from_below(b, k):
        ag_copy(True, b, k, above).wait_recv()
        ag_copy(True, b, k, above).start()

    def arrive(i, k):
        far = (i + 1) // 2
        if i % 2:
            @pl.when(2 * zeta >= i)
            def _():
                from_below(zeta - far, k)
                from_above(zeta + far, k)

        @pl.when(2 * zeta < i)
        def _():
            from_above(i, k)

    def step_block(i):
        if i == 0:
            return z
        near = lax.div(2 * zeta - i + ns, ns)
        side = zeta - (i + 1) // 2 if i % 2 else zeta + i // 2
        return phys(near * side + (1 - near) * i)

    tri = (
        lax.broadcasted_iota(jnp.int32, (tok, tok), 0) < lax.broadcasted_iota(jnp.int32, (tok, tok), 1)
    ).astype(F32).astype(BF16)
    slot_of = lax.broadcasted_iota(jnp.int32, (cap, tok), 0).astype(F32)
    mask_rows = -(-local_count // 8) * 8
    row_of = lax.broadcasted_iota(jnp.int32, (mask_rows, tok), 0)
    columns = local_count * piece

    def dispatch(s):
        info = meta_all[s]
        masks, weights = [], []
        mask_all = jnp.zeros((mask_rows, tok), F32)
        for l in range(local_count):
            eid = lax.div(z * columns + l * piece, FFE).astype(F32)
            hit = (info[:top] == eid).astype(F32)
            mask = jnp.sum(hit, axis=0, keepdims=True)
            masks.append(mask)
            weights.append(jnp.sum(hit * info[top : 2 * top], axis=0, keepdims=True))
            mask_all = jnp.where(row_of == l, mask, mask_all)
        position = mm(mask_all.astype(BF16), tri)
        picks = []
        for l in range(local_count):
            pick = jnp.where((slot_of == position[l : l + 1]) & (masks[l] > 0.5), 1.0, 0.0)
            picks.append(pick.astype(BF16))
            comb[s, pl.ds(l * cap, cap), :] = (pick * weights[l]).astype(BF16)
        stacked = jnp.concatenate(picks, axis=0) if local_count > 1 else picks[0]
        gathered = mm(stacked, x_all[s]).astype(BF16)
        for l in range(local_count):
            rows[l] = gathered[l * cap : (l + 1) * cap]

    units = local_count + 1

    def refs(i, u):
        if u == 0:
            return (
                s_part.at[i % 2], s_core_in.at[i], s_x_out.at[i], s_x_in.at[i], s_hid.at[step_block(i)]
            )
        e = u - 1
        return part.at[i % 2, e], core_in.at[i, e], x_out.at[i, e], x_in.at[i, e], hid.at[i, e]

    def along(u, start, size, lead):
        step = pl.ds(pl.multiple_of(start, size), size)
        return lead + ((step, slice(None)) if u == 0 else (slice(None), step))

    def extent(u):
        return tok if u == 0 else piece

    def first(i, u):
        p, ci = refs(i, u)[:2]
        if u == 0:
            if i == 0:
                sin_load.wait()
            block = x_all[step_block(i)]
            for g in range(2):
                p[g] = mm(block, sin_w[g], 1, 1).astype(BF16)
        else:
            e = u - 1
            lhs = rows[e]
            if i == 0:
                gate_loads[e].wait()
            p[0] = mm(lhs, gate_w[e]).astype(BF16)
            if i == 0:
                up_loads[e].wait()
            p[1] = mm(lhs, up_w[e]).astype(BF16)
        half = extent(u) // 2
        theirs = along(u, peer_c * half, half, (slice(None),))
        copy = remote(p.at[theirs], ci, core_sem, (i, u), {"tensor": peer_t})
        copy.start()
        return copy

    def chunk(i, u, which):
        p, ci = refs(i, u)[:2]
        half = extent(u) // 2
        q = half // nx
        sums = []
        for g in range(2):
            mine = p[along(u, c * half + which * q, q, (g,))].astype(F32)
            sums.append(mine + ci[along(u, which * q, q, (g,))].astype(F32))
        return sums

    def second(i, u, core_copy):
        _, _, xo, xi, _ = refs(i, u)
        core_copy.wait()
        copies = []
        for k in range(1, nx):
            other = lax.rem(x + k, nx)
            sums = chunk(i, u, other)
            for g in range(2):
                xo[k - 1, g] = sums[g].astype(BF16)
            copy = remote(xo.at[k - 1], xi.at[k - 1], x_sem, (i, u, k - 1), {"tensor": 2 * other + c})
            copy.start()
            copies.append(copy)
        return copies

    def hid_part(i, u, which):
        half = extent(u) // 2
        q = half // nx
        return refs(i, u)[4].at[along(u, c * half + which * q, q, ())]

    def third(i, u, x_copies):
        xi = refs(i, u)[3]
        sums = chunk(i, u, x)
        for k in range(1, nx):
            x_copies[k - 1].wait()
            for g in range(2):
                sums[g] = sums[g] + xi[k - 1, g].astype(F32)
        gate, up = sums
        value = (gate / (1.0 + jnp.exp(-gate)) * up).astype(BF16)
        ref = hid_part(i, u, x)
        ref[...] = value
        x_sends = []
        for k in range(1, nx):
            where = {"tensor": 2 * lax.rem(x + k, nx) + c}
            copy = remote(ref, ref, hx_sem, (i, u, k - 1), where)
            copy.start()
            x_sends.append(copy)
        copy = remote(ref, ref, hc_sem, (i, u, 0), {"tensor": peer_t})
        copy.start()
        return x_sends, [copy]

    def fourth(i, u, x_sends, core_sends):
        for k in range(1, nx):
            x_sends[k - 1].wait()
            ref = hid_part(i, u, lax.rem(x + nx - k, nx))
            copy = remote(ref, ref, hc_sem, (i, u, k), {"tensor": peer_t})
            copy.start()
            core_sends.append(copy)
        return core_sends

    def fifth(i, u, core_sends):
        for copy in core_sends:
            copy.wait()
        if u > 0:
            e = u - 1
            if i == 0:
                down_loads[e].wait()
            made[step_block(i), pl.ds(e * cap, cap), :] = mm(hid[i, e], down_w[e]).astype(BF16)
        elif i == 0:
            sdown_load.wait()

    parts = width // cw

    def contribution(b, k):
        span = pl.ds(k * cw, cw)
        return mm(comb[b], made[b, :, span], 0, 0) + mm(s_hid[b], sdown_w[:, span])

    def rs_copy(upward, b, k, where):
        d = mir if upward else 1 - mir
        block = phys(b)
        slot = block + 1 - d
        span = pl.ds(k * cw, cw)
        return remote(
            x_all.at[block, :, span], rs_in.at[slot, :, span], rs_sem, (slot, k), {"expert": where}
        )

    def arrived(upward, b, k):
        rs_copy(upward, b, k, above).wait_recv()
        d = mir if upward else 1 - mir
        return rs_in[phys(b) + 1 - d, :, pl.ds(k * cw, cw)].astype(F32)

    def originate(r):
        @pl.when(zeta == 0)
        def _():
            for k in range(parts):
                x_all[phys(r), :, pl.ds(k * cw, cw)] = contribution(phys(r), k).astype(BF16)
                rs_copy(True, r, k, above).start()

    def relay(upward, b, k):
        value = contribution(phys(b), k)
        total = value + arrived(upward, b, k)
        x_all[phys(b), :, pl.ds(k * cw, cw)] = total.astype(BF16)
        rs_copy(upward, b, k, above if upward else below).start()

    state = {}

    def run(name, i, u):
        if name == "A":
            state[i, u] = first(i, u)
        elif name == "B":
            state[i, u] = second(i, u, state[i, u])
        elif name == "C":
            state[i, u] = third(i, u, state[i, u])
        elif name == "D":
            state[i, u] = fourth(i, u, *state[i, u])
        else:
            fifth(i, u, state[i, u])

    mid = units // 2
    for i in range(ns):
        if i > 0:
            for k in range(pieces):
                if k == 0:
                    pl.when(zeta == 0)(functools.partial(arrive, i, k))
                else:
                    arrive(i, k)
            if i == 1:
                for copy in meta_copies:
                    copy.wait()
        dispatch(step_block(i))
        behind = []
        if i > 0:
            behind = [("D", u) for u in range(units)] + [("E", u) for u in range(units)]
        per = -(-len(behind) // max(1, units - 1))
        for u in range(units):
            run("A", i, u)
            if u > 0:
                run("B", i, u - 1)
                for name, v in behind[(u - 1) * per : u * per]:
                    run(name, i - 1, v)
            if u >= 3:
                run("C", i, u - 3)
            if u == mid and i + 1 < ns:
                pl.when(zeta > 0)(functools.partial(arrive, i + 1, 0))
        if i > 1:
            originate(i - 1)
        run("B", i, units - 1)
        tail = list(range(max(0, units - 3), units))
        if i + 1 < ns:
            for u in tail:
                run("C", i, u)
        else:
            for u in tail:
                run("C", i, u)
                run("D", i, u - tail[0])
            for u in range(units):
                if u + len(tail) < units:
                    run("D", i, u + len(tail))
                run("E", i, u)
    originate(ns - 1)

    @pl.when(zeta > 0)
    def _():
        for k in range(pieces):
            ag_copy(True, zeta, k, above).wait_send()
            ag_copy(False, zeta, k, below).wait_send()
            for b in range(ns):
                @pl.when(b < zeta)
                def _():
                    ag_copy(True, b, k, above).wait_send()

                @pl.when(b > zeta)
                def _():
                    ag_copy(False, b, k, below).wait_send()

    for r in range(1, ns):
        for k in range(parts + 2):
            if k < parts:
                pl.when((zeta > 0) & (zeta < r))(functools.partial(relay, True, r, k))
            if k >= 2:
                pl.when(zeta > ns - 1 - r)(functools.partial(relay, False, ns - 1 - r, k - 2))

    for k in range(parts):
        span = pl.ds(k * cw, cw)
        value = contribution(z, k) + arrived(False, zeta, k)

        @pl.when(zeta == 0)
        def _():
            out[:, span] = value.astype(BF16)

        @pl.when(zeta > 0)
        def _():
            out[:, span] = (value + arrived(True, zeta, k)).astype(BF16)

    @pl.when(zeta == 0)
    def _():
        for k in range(pieces):
            ag_copy(True, zeta, k, above).wait_send()

    for b in range(ns):
        for k in range(parts):
            @pl.when(zeta < b)
            def _():
                rs_copy(True, b, k, above).wait_send()

            @pl.when(zeta > b)
            def _():
                rs_copy(False, b, k, above).wait_send()


def local(tokens, choices, affinity, expert_gate, expert_up, expert_down, shared_in, shared_down):
    tok, width = tokens.shape
    top = choices.shape[1]
    ns, nt = lax.axis_size("expert"), lax.axis_size("tensor")
    nx = nt // 2
    piece = min(FFE, expert_gate.shape[1])
    local_count = expert_gate.shape[1] // piece
    hs = shared_in.shape[1]
    hops = ns // 2
    slots = min(3, local_count)
    sigmoids = jax.nn.sigmoid(affinity)
    mix = 2.5 * sigmoids / jnp.sum(sigmoids, axis=1, keepdims=True)
    meta = jnp.concatenate([choices.astype(F32).T, mix.T], axis=0)
    rows = ns * CAP
    srows = ns * tok
    units = local_count + 1
    dims = (ns, nx, local_count, piece, tok, CAP, top)
    hbm = pl.BlockSpec(memory_space=pl.ANY)
    sem = pltpu.SemaphoreType.DMA
    scratch = [
        pltpu.VMEM((ns, tok, width), BF16),
        pltpu.VMEM((ns,) + meta.shape, F32),
        pltpu.VMEM((slots, width, piece), BF16),
        pltpu.VMEM((slots, width, piece), BF16),
        pltpu.VMEM((local_count, piece, width), BF16),
        pltpu.VMEM(shared_in.shape, BF16),
        pltpu.VMEM(shared_down.shape, BF16),
        pltpu.VMEM((local_count, ns, CAP, width), BF16),
        pltpu.VMEM((ns, local_count * CAP, tok), BF16),
        pltpu.VMEM((local_count, 2, rows, piece), BF16),
        pltpu.VMEM((local_count, 2, rows // 2, piece), BF16),
        pltpu.VMEM((local_count, nx - 1, 2, rows // nt, piece), BF16),
        pltpu.VMEM((local_count, nx - 1, 2, rows // nt, piece), BF16),
        pltpu.VMEM((local_count, rows, piece), BF16),
        pltpu.VMEM((2, srows, hs), BF16),
        pltpu.VMEM((2, srows // 2, hs), BF16),
        pltpu.VMEM((nx - 1, 2, srows // nt, hs), BF16),
        pltpu.VMEM((nx - 1, 2, srows // nt, hs), BF16),
        pltpu.VMEM((srows, hs), BF16),
        pltpu.VMEM((2, hops, tok, width), BF16),
        pltpu.VMEM((2, hops, tok, width), BF16),
        sem((4,)),
        sem((local_count,)),
        sem((local_count,)),
        sem((local_count,)),
        sem((2, ns - 1)),
        sem((2, 2, hops)),
        sem((2, units)),
        sem((2, units, nx - 1)),
        sem((2, units, nx - 1)),
        sem((2, units, nx)),
        sem((2, 2, hops)),
    ]
    return pl.pallas_call(
        functools.partial(layer, dims),
        out_shape=jax.ShapeDtypeStruct((tok, width), BF16),
        in_specs=[hbm] * 7,
        out_specs=pl.BlockSpec(memory_space=pltpu.VMEM),
        scratch_shapes=scratch,
        compiler_params=pltpu.CompilerParams(
            collective_id=0, has_side_effects=True, vmem_limit_bytes=60 * 1024 * 1024
        ),
        name="moe_layer",
    )(tokens, meta, expert_gate, expert_up, expert_down, shared_in, shared_down)


def line_local(tokens, choices, affinity, expert_gate, expert_up, expert_down, shared_in, shared_down):
    tok, width = tokens.shape
    top = choices.shape[1]
    ns, nt = lax.axis_size("expert"), lax.axis_size("tensor")
    nx = nt // 2
    piece = min(FFE, expert_gate.shape[1])
    local_count = expert_gate.shape[1] // piece
    hs = shared_in.shape[1]
    pieces = 2
    cw = 256 if width % 256 == 0 else 128
    sigmoids = jax.nn.sigmoid(affinity)
    mix = 2.5 * sigmoids / jnp.sum(sigmoids, axis=1, keepdims=True)
    meta = jnp.concatenate([choices.astype(F32).T, mix.T], axis=0)
    units = local_count + 1
    dims = (ns, nx, local_count, piece, tok, CAP, top, pieces, cw)
    hbm = pl.BlockSpec(memory_space=pl.ANY)
    sem = pltpu.SemaphoreType.DMA
    scratch = [
        pltpu.VMEM((ns, tok, width), BF16),
        pltpu.VMEM((ns,) + meta.shape, F32),
        pltpu.VMEM((local_count, width, piece), BF16),
        pltpu.VMEM((local_count, width, piece), BF16),
        pltpu.VMEM((local_count, piece, width), BF16),
        pltpu.VMEM(shared_in.shape, BF16),
        pltpu.VMEM(shared_down.shape, BF16),
        pltpu.VMEM((local_count, CAP, width), BF16),
        pltpu.VMEM((ns, local_count * CAP, width), BF16),
        pltpu.VMEM((ns, local_count * CAP, tok), BF16),
        pltpu.VMEM((2, local_count, 2, CAP, piece), BF16),
        pltpu.VMEM((ns, local_count, 2, CAP, piece // 2), BF16),
        pltpu.VMEM((ns, local_count, nx - 1, 2, CAP, piece // nt), BF16),
        pltpu.VMEM((ns, local_count, nx - 1, 2, CAP, piece // nt), BF16),
        pltpu.VMEM((ns, local_count, CAP, piece), BF16),
        pltpu.VMEM((2, 2, tok, hs), BF16),
        pltpu.VMEM((ns, 2, tok // 2, hs), BF16),
        pltpu.VMEM((ns, nx - 1, 2, tok // nt, hs), BF16),
        pltpu.VMEM((ns, nx - 1, 2, tok // nt, hs), BF16),
        pltpu.VMEM((ns, tok, hs), BF16),
        pltpu.VMEM((ns + 1, tok, width), BF16),
        sem((4,)),
        sem((local_count,)),
        sem((local_count,)),
        sem((local_count,)),
        sem((2, ns - 1)),
        sem((2, 2, ns, pieces)),
        sem((2, ns, units)),
        sem((2, ns, units, nx - 1)),
        sem((2, ns, units, nx - 1)),
        sem((2, ns, units, nx)),
        sem((2, ns + 1, width // cw)),
    ]
    return pl.pallas_call(
        functools.partial(line_layer, dims),
        out_shape=jax.ShapeDtypeStruct((tok, width), BF16),
        in_specs=[hbm] * 7,
        out_specs=pl.BlockSpec(memory_space=pltpu.VMEM),
        scratch_shapes=scratch,
        compiler_params=pltpu.CompilerParams(
            collective_id=0, has_side_effects=True, vmem_limit_bytes=65400 * 1024
        ),
        name="moe_line",
    )(tokens, meta, expert_gate, expert_up, expert_down, shared_in, shared_down)


def choose(tokens, choices, affinity, expert_gate, *rest):
    tok = tokens.shape[0]
    ns, nt = lax.axis_size("expert"), lax.axis_size("tensor")
    piece = min(FFE, expert_gate.shape[1])
    fits = ns % 2 == 0 and piece % (128 * nt) == 0 and tok % (16 * nt) == 0 and expert_gate.shape[1] % piece == 0
    which = line_local if fits else local
    return which(tokens, choices, affinity, expert_gate, *rest)


def solution(mesh):
    placed = (
        P(("groups", "expert"), "tensor"),
        P(("groups", "expert"), None),
        P(("groups", "expert"), None),
        P("tensor", "expert"),
        P("tensor", "expert"),
        P("expert", "tensor"),
        P(None, "expert", "tensor"),
        P("expert", "tensor"),
    )
    return jax.shard_map(
        choose,
        mesh=mesh,
        in_specs=placed,
        out_specs=P(("groups", "expert"), "tensor"),
        check_vma=False,
    )
```

profile of v0, /device:TPU:0, one launch (start us, length us, event | category | flops | bytes accessed | tf_op | source)
XLA Modules:
  0.0 107.3 jit_solution(345971836348918027)
XLA Ops:
  0.0 0.7 fusion
  0.7 0.7 divide_bitcast_fusion
  1.4 0.7 convert_bitcast_fusion
  2.1 0.6 pad_maximum_fusion.meta
  2.7 102.8 %moe_line.1 = bf16[128,1792]{1,0:T(8,128)(2,1)} custom-call(bf16[128,1792]{1,0:T(8,128)(2,1)} %tokens.1, f32[8,128]{1,0:T(8,128)} %pad_maximum_fusion.meta, bf16[1792,4096]{1,0:T(8,128)(2,1)} %gate_hbm.1, bf16[1792,4096]{1,0:T(8,128)(2,1)} %up_hbm.1, bf16[4096,1792]{1,0:T(8,128)(2,1)} %down_hbm.1, bf16[2,256,1792]{2,1,0:T(8,128)(2,1)} %sin_hbm.1, ...), custom_call_target="tpu_custom_call" | custom-call | tf_op jit(solution)/shard_map/moe_line/pallas_call | solution.py:822
  105.5 1.8 %copy.10 = bf16[128,1792]{1,0:T(8,128)(2,1)} copy(bf16[128,1792]{1,0:T(8,128)(2,1)} %moe_line.1) | data formatting | bytes 917504
where the time goes:
time: 108 us; the launch traced here: 107 us
  Pallas kernels  103 us (95%)
  other arithmetic  2.69 us (2%)
  local copies, waits for them, and re-layouts  1.82 us (2%)
    pallas_call x1, Pallas kernels, line_local(): pl.pallas_call(functools.partial(line_layer, dims), out_shape=jax.ShapeDt...  103 us

commit v1 on v0

--- a/solution.py
+++ b/solution.py
@@ -305,10 +305,10 @@
 
 
 def line_layer(
-    dims, tokens, meta, gate_hbm, up_hbm, down_hbm, sin_hbm, sdown_hbm, out,
-    x_all, meta_all, gate_w, up_w, down_w, sin_w, sdown_w, rows, made, comb,
+    dims, tokens, choices, affinity, gate_hbm, up_hbm, down_hbm, sin_hbm, sdown_hbm, out,
+    x_all, choice_v, affinity_v, out_v, meta_all, gate_w, up_w, down_w, sin_w, sdown_w, rows, made, comb,
     part, core_in, x_out, x_in, hid, s_part, s_core_in, s_x_out, s_x_in, s_hid, rs_in,
-    load_sem, gate_sem, up_sem, down_sem, meta_sem, ag_sem, core_sem, x_sem, hx_sem, hc_sem, rs_sem,
+    load_sem, gate_sem, up_sem, down_sem, meta_sem, ag_sem, core_sem, x_sem, hx_sem, hc_sem, rs_sem, rs_half_sem, out_sem,
 ):
     ns, nx, local_count, piece, tok, cap, top, pieces, cw = dims
     width = x_all.shape[2]
@@ -336,9 +336,11 @@
         )
 
     own_tok = pltpu.make_async_copy(tokens, x_all.at[z], load_sem.at[0])
-    own_meta = pltpu.make_async_copy(meta, meta_all.at[z], load_sem.at[1])
+    own_choice = pltpu.make_async_copy(choices, choice_v, load_sem.at[1])
+    own_affinity = pltpu.make_async_copy(affinity, affinity_v, load_sem.at[4])
+    own_choice.start()
+    own_affinity.start()
     own_tok.start()
-    own_meta.start()
     barrier = pltpu.get_barrier_semaphore()
     for k in range(1, ns):
         pl.semaphore_signal(barrier, inc=1, device_id={"expert": zoff(k)}, device_id_type=MESH)
@@ -363,22 +365,28 @@
     down_loads = [
         pltpu.make_async_copy(down_hbm.at[cols(e), :], down_w.at[e], down_sem.at[e]) for e in range(local_count)
     ]
-    sin_load.start()
-    for e in range(local_count):
-        gate_loads[e].start()
-        up_loads[e].start()
-    for e in range(local_count):
-        down_loads[e].start()
-    sdown_load.start()
+    queue = [load for pair in zip(gate_loads, up_loads) for load in pair] + [sin_load] + down_loads + [sdown_load]
+
+    def load_next(count):
+        for load in queue[:count]:
+            load.start()
+        del queue[:count]
+
+    load_next(3)
+    own_choice.wait()
+    own_affinity.wait()
+    sigmoids = jax.nn.sigmoid(affinity_v[...])
+    mix = 2.5 * sigmoids / jnp.sum(sigmoids, axis=0, keepdims=True)
+    meta_all[z, :top] = choice_v[...].astype(F32)
+    meta_all[z, top:] = mix
     own_tok.wait()
-    own_meta.wait()
     pl.semaphore_wait(barrier, (ns - 1) + (nx - 1) + 1)
 
     def ag_copy(upward, b, k, where):
         d = mir if upward else 1 - mir
         block = phys(b)
         ref = x_all.at[block, pl.ds(k * spread, spread), :]
-        return remote(ref, ref, ag_sem, (d, block, k), {"expert": where})
+        return remote(ref, ref, ag_sem, (block + d, k), {"expert": where})
 
     for k in range(pieces):
         ag_copy(True, zeta, k, above).start()
@@ -456,40 +464,44 @@
     units = local_count + 1
 
     def refs(i, u):
-        if u == 0:
+        if u == local_count:
             return (
                 s_part.at[i % 2], s_core_in.at[i], s_x_out.at[i], s_x_in.at[i], s_hid.at[step_block(i)]
             )
-        e = u - 1
-        return part.at[i % 2, e], core_in.at[i, e], x_out.at[i, e], x_in.at[i, e], hid.at[i, e]
+        return part.at[i % 2, u], core_in.at[i, u], x_out.at[i, u], x_in.at[i, u], hid.at[u, i]
 
     def along(u, start, size, lead):
         step = pl.ds(pl.multiple_of(start, size), size)
-        return lead + ((step, slice(None)) if u == 0 else (slice(None), step))
+        return lead + ((step, slice(None)) if u == local_count else (slice(None), step))
+
+    def turn(i):
+        return 1 + (i - 1) % 2 if i else 0
 
     def extent(u):
-        return tok if u == 0 else piece
+        return tok if u == local_count else piece
 
     def first(i, u):
         p, ci = refs(i, u)[:2]
-        if u == 0:
+        if u == local_count:
             if i == 0:
                 sin_load.wait()
             block = x_all[step_block(i)]
             for g in range(2):
                 p[g] = mm(block, sin_w[g], 1, 1).astype(BF16)
         else:
-            e = u - 1
+            e = u
             lhs = rows[e]
             if i == 0:
                 gate_loads[e].wait()
+                load_next(1)
             p[0] = mm(lhs, gate_w[e]).astype(BF16)
             if i == 0:
                 up_loads[e].wait()
+                load_next(1)
             p[1] = mm(lhs, up_w[e]).astype(BF16)
         half = extent(u) // 2
         theirs = along(u, peer_c * half, half, (slice(None),))
-        copy = remote(p.at[theirs], ci, core_sem, (i, u), {"tensor": peer_t})
+        copy = remote(p.at[theirs], ci, core_sem, (i % 2, u), {"tensor": peer_t})
         copy.start()
         return copy
 
@@ -512,7 +524,7 @@
             sums = chunk(i, u, other)
             for g in range(2):
                 xo[k - 1, g] = sums[g].astype(BF16)
-            copy = remote(xo.at[k - 1], xi.at[k - 1], x_sem, (i, u, k - 1), {"tensor": 2 * other + c})
+            copy = remote(xo.at[k - 1], xi.at[k - 1], x_sem, (i % 2, u, k - 1), {"tensor": 2 * other + c})
             copy.start()
             copies.append(copy)
         return copies
@@ -536,10 +548,10 @@
         x_sends = []
         for k in range(1, nx):
             where = {"tensor": 2 * lax.rem(x + k, nx) + c}
-            copy = remote(ref, ref, hx_sem, (i, u, k - 1), where)
+            copy = remote(ref, ref, hx_sem, (i % 2, u, k - 1), where)
             copy.start()
             x_sends.append(copy)
-        copy = remote(ref, ref, hc_sem, (i, u, 0), {"tensor": peer_t})
+        copy = remote(ref, ref, hc_sem, (turn(i), u, 0), {"tensor": peer_t})
         copy.start()
         return x_sends, [copy]
 
@@ -547,21 +559,27 @@
         for k in range(1, nx):
             x_sends[k - 1].wait()
             ref = hid_part(i, u, lax.rem(x + nx - k, nx))
-            copy = remote(ref, ref, hc_sem, (i, u, k), {"tensor": peer_t})
+            copy = remote(ref, ref, hc_sem, (turn(i), u, k), {"tensor": peer_t})
             copy.start()
             core_sends.append(copy)
         return core_sends
 
-    def fifth(i, u, core_sends):
-        for copy in core_sends:
-            copy.wait()
-        if u > 0:
-            e = u - 1
-            if i == 0:
-                down_loads[e].wait()
-            made[step_block(i), pl.ds(e * cap, cap), :] = mm(hid[i, e], down_w[e]).astype(BF16)
-        elif i == 0:
-            sdown_load.wait()
+    def fifth(i, u):
+        span = (0, 1) if i == 1 else (i,)
+        for j in span:
+            for copy in state[j, u]:
+                copy.wait()
+        if u == local_count:
+            if i == 1:
+                sdown_load.wait()
+            return
+        if i == 1:
+            down_loads[u].wait()
+        count = len(span)
+        lhs = hid[u, pl.ds(span[0], count)].reshape(count * cap, piece)
+        result = mm(lhs, down_w[u]).astype(BF16)
+        for n, j in enumerate(span):
+            made[step_block(j), pl.ds(u * cap, cap), :] = result[n * cap : (n + 1) * cap]
 
     parts = width // cw
 
@@ -569,32 +587,42 @@
         span = pl.ds(k * cw, cw)
         return mm(comb[b], made[b, :, span], 0, 0) + mm(s_hid[b], sdown_w[:, span])
 
-    def rs_copy(upward, b, k, where):
+    half_rows = tok // 2
+
+    def spans(end):
+        return [pl.ds(0, half_rows), pl.ds(half_rows, half_rows)] if end else [pl.ds(0, tok)]
+
+    def rs_copy(upward, b, k, h, end, where):
         d = mir if upward else 1 - mir
         block = phys(b)
         slot = block + 1 - d
-        span = pl.ds(k * cw, cw)
-        return remote(
-            x_all.at[block, :, span], rs_in.at[slot, :, span], rs_sem, (slot, k), {"expert": where}
-        )
-
-    def arrived(upward, b, k):
-        rs_copy(upward, b, k, above).wait_recv()
+        span = (spans(end)[h], pl.ds(k * cw, cw))
+        sems, index = (rs_half_sem, (d, k)) if h else (rs_sem, (slot, k))
+        return remote(x_all.at[(block,) + span], rs_in.at[(slot,) + span], sems, index, {"expert": where})
+
+    def arrived(upward, b, k, h, end):
+        rs_copy(upward, b, k, h, end, above).wait_recv()
         d = mir if upward else 1 - mir
-        return rs_in[phys(b) + 1 - d, :, pl.ds(k * cw, cw)].astype(F32)
-
-    def originate(r):
+        return rs_in[phys(b) + 1 - d, spans(end)[h], pl.ds(k * cw, cw)].astype(F32)
+
+    early = min(3, parts)
+
+    def originate(r, span):
         @pl.when(zeta == 0)
         def _():
-            for k in range(parts):
+            for k in span:
                 x_all[phys(r), :, pl.ds(k * cw, cw)] = contribution(phys(r), k).astype(BF16)
-                rs_copy(True, r, k, above).start()
+                end = r + 1 == ns
+                for h in range(len(spans(end))):
+                    rs_copy(True, r, k, h, end, above).start()
 
     def relay(upward, b, k):
         value = contribution(phys(b), k)
-        total = value + arrived(upward, b, k)
-        x_all[phys(b), :, pl.ds(k * cw, cw)] = total.astype(BF16)
-        rs_copy(upward, b, k, above if upward else below).start()
+        end = b + 1 == ns if upward else b == 0
+        for h, side in enumerate(spans(end)):
+            total = value[side.start : side.start + side.size] + arrived(upward, b, k, h, end)
+            x_all[phys(b), side, pl.ds(k * cw, cw)] = total.astype(BF16)
+            rs_copy(upward, b, k, h, end, above if upward else below).start()
 
     state = {}
 
@@ -608,50 +636,94 @@
         elif name == "D":
             state[i, u] = fourth(i, u, *state[i, u])
         else:
-            fifth(i, u, state[i, u])
-
-    mid = units // 2
+            fifth(i, u)
+
+    def inner(i, k):
+        if i < ns:
+            pl.when(zeta > 0)(functools.partial(arrive, i, k))
+
+    def outer(i, k):
+        pl.when(zeta == 0)(functools.partial(arrive, i, k))
+
+    last = units - 1
     for i in range(ns):
-        if i > 0:
-            for k in range(pieces):
-                if k == 0:
-                    pl.when(zeta == 0)(functools.partial(arrive, i, k))
-                else:
-                    arrive(i, k)
-            if i == 1:
-                for copy in meta_copies:
-                    copy.wait()
+        if i == 1:
+            outer(1, 0)
+            arrive(1, 1)
+            for copy in meta_copies:
+                copy.wait()
+        elif i > 1:
+            outer(i, 0)
+            outer(i, 1)
         dispatch(step_block(i))
-        behind = []
-        if i > 0:
-            behind = [("D", u) for u in range(units)] + [("E", u) for u in range(units)]
-        per = -(-len(behind) // max(1, units - 1))
         for u in range(units):
             run("A", i, u)
             if u > 0:
                 run("B", i, u - 1)
-                for name, v in behind[(u - 1) * per : u * per]:
-                    run(name, i - 1, v)
-            if u >= 3:
-                run("C", i, u - 3)
-            if u == mid and i + 1 < ns:
-                pl.when(zeta > 0)(functools.partial(arrive, i + 1, 0))
-        if i > 1:
-            originate(i - 1)
-        run("B", i, units - 1)
-        tail = list(range(max(0, units - 3), units))
+            if i == 0:
+                if u >= 2:
+                    run("C", i, u - 2)
+                if u == 2:
+                    inner(1, 0)
+            else:
+                if u == 0:
+                    inner(i + 1, 1)
+                if i < 3 and u < 2:
+                    for v in range(-(-len(late) // (2 - u))):
+                        run("C", i - 1, late.pop(0))
+                if i > 2 and u == 0:
+                    for v in range(units - 2):
+                        run("D", i - 1, v)
+                    relays = [units - 2, last]
+                elif u == 1 and i < 3:
+                    run("D", i - 1, 0)
+                    run("D", i - 1, 1)
+                    relays = list(range(2, units))
+                elif u >= 3 or (i > 2 and u > 0):
+                    for v in range(-(-len(relays) // (units - u)) if i < 3 else 1):
+                        if relays:
+                            run("D", i - 1, relays.pop(0))
+                if u >= 3:
+                    run("C", i, u - 3)
+        if i > 0:
+            inner(i + 2, 0)
+        if i == 0:
+            load_next(len(queue))
+            run("B", 0, last)
+            late = [units - 2, last]
+            continue
+        rest = list(range(units - 3, last))
+        if i == 1:
+            run("B", i, last)
+            late = rest + [last]
+            if i + 1 < ns:
+                continue
+            rest = late
+        else:
+            for u in range(units):
+                run("E", i - 1, u)
+                if u == 0:
+                    run("B", i, last)
+                elif rest and u < last:
+                    run("C", i, rest.pop(0))
+            originate(i - 1, range(early if i + 1 == ns else parts))
+            rest.append(last)
         if i + 1 < ns:
-            for u in tail:
+            for u in rest:
                 run("C", i, u)
-        else:
-            for u in tail:
-                run("C", i, u)
-                run("D", i, u - tail[0])
-            for u in range(units):
-                if u + len(tail) < units:
-                    run("D", i, u + len(tail))
-                run("E", i, u)
-    originate(ns - 1)
+    for u in rest:
+        run("C", ns - 1, u)
+    for u in range(units):
+        if u == last:
+            run("E", ns - 1, u - 2)
+        run("D", ns - 1, u)
+        if 2 <= u < last:
+            run("E", ns - 1, u - 2)
+    run("E", ns - 1, last - 1)
+    run("E", ns - 1, last)
+    originate(ns - 1, range(parts))
+    if ns > 2:
+        originate(ns - 2, range(early, parts))
 
     @pl.when(zeta > 0)
     def _():
@@ -667,39 +739,50 @@
                 def _():
                     ag_copy(False, b, k, below).wait_send()
 
-    for r in range(1, ns):
-        for k in range(parts + 2):
-            if k < parts:
-                pl.when((zeta > 0) & (zeta < r))(functools.partial(relay, True, r, k))
-            if k >= 2:
-                pl.when(zeta > ns - 1 - r)(functools.partial(relay, False, ns - 1 - r, k - 2))
-
-    for k in range(parts):
-        span = pl.ds(k * cw, cw)
-        value = contribution(z, k) + arrived(False, zeta, k)
-
-        @pl.when(zeta == 0)
-        def _():
-            out[:, span] = value.astype(BF16)
-
-        @pl.when(zeta > 0)
-        def _():
-            out[:, span] = (value + arrived(True, zeta, k)).astype(BF16)
+    order = [(r, k) for r in range(2, ns - 2) for k in range(parts)]
+    if ns > 3:
+        order += [(ns - 2, k) for k in range(early)]
+    order += [(ns - 1, k) for k in range(parts)]
+    if ns > 3:
+        order += [(ns - 2, k) for k in range(early, parts)]
+    for n in range(len(order) + 2):
+        if n < len(order):
+            r, k = order[n]
+            pl.when((zeta > 0) & (zeta < r))(functools.partial(relay, True, r, k))
+        if n >= 2:
+            r, k = order[n - 2]
+            if r > ns // 2:
+                pl.when(zeta > ns - 1 - r)(functools.partial(relay, False, ns - 1 - r, k))
+
+    def finish(inside):
+        for k in range(parts):
+            span = pl.ds(k * cw, cw)
+            value = contribution(z, k)
+            for h, side in enumerate(spans(not inside)):
+                total = value[side.start : side.start + side.size] + arrived(False, zeta, k, h, not inside)
+                if inside:
+                    total = total + arrived(True, zeta, k, h, False)
+                out_v[side, span] = total.astype(BF16)
+            pltpu.make_async_copy(out_v.at[:, span], out.at[:, span], out_sem).start()
+
+    pl.when(zeta == 0)(functools.partial(finish, False))
+    pl.when(zeta > 0)(functools.partial(finish, True))
 
     @pl.when(zeta == 0)
     def _():
         for k in range(pieces):
             ag_copy(True, zeta, k, above).wait_send()
 
+    def sent(upward, b):
+        end = b + 1 == ns if upward else b == 0
+        for k in range(parts):
+            for h in range(len(spans(end))):
+                rs_copy(upward, b, k, h, end, above).wait_send()
+
     for b in range(ns):
-        for k in range(parts):
-            @pl.when(zeta < b)
-            def _():
-                rs_copy(True, b, k, above).wait_send()
-
-            @pl.when(zeta > b)
-            def _():
-                rs_copy(False, b, k, above).wait_send()
+        pl.when(zeta < b)(functools.partial(sent, True, b))
+        pl.when(zeta > b)(functools.partial(sent, False, b))
+    pltpu.make_async_copy(out_v, out, out_sem).wait()
 
 
 def local(tokens, choices, affinity, expert_gate, expert_up, expert_down, shared_in, shared_down):
@@ -778,16 +861,16 @@
     hs = shared_in.shape[1]
     pieces = 2
     cw = 256 if width % 256 == 0 else 128
-    sigmoids = jax.nn.sigmoid(affinity)
-    mix = 2.5 * sigmoids / jnp.sum(sigmoids, axis=1, keepdims=True)
-    meta = jnp.concatenate([choices.astype(F32).T, mix.T], axis=0)
     units = local_count + 1
     dims = (ns, nx, local_count, piece, tok, CAP, top, pieces, cw)
     hbm = pl.BlockSpec(memory_space=pl.ANY)
     sem = pltpu.SemaphoreType.DMA
     scratch = [
         pltpu.VMEM((ns, tok, width), BF16),
-        pltpu.VMEM((ns,) + meta.shape, F32),
+        pltpu.VMEM((top, tok), jnp.int32),
+        pltpu.VMEM((top, tok), F32),
+        pltpu.VMEM((tok, width), BF16),
+        pltpu.VMEM((ns, 2 * top, tok), F32),
         pltpu.VMEM((local_count, width, piece), BF16),
         pltpu.VMEM((local_count, width, piece), BF16),
         pltpu.VMEM((local_count, piece, width), BF16),
@@ -800,36 +883,38 @@
         pltpu.VMEM((ns, local_count, 2, CAP, piece // 2), BF16),
         pltpu.VMEM((ns, local_count, nx - 1, 2, CAP, piece // nt), BF16),
         pltpu.VMEM((ns, local_count, nx - 1, 2, CAP, piece // nt), BF16),
-        pltpu.VMEM((ns, local_count, CAP, piece), BF16),
+        pltpu.VMEM((local_count, ns, CAP, piece), BF16),
         pltpu.VMEM((2, 2, tok, hs), BF16),
         pltpu.VMEM((ns, 2, tok // 2, hs), BF16),
         pltpu.VMEM((ns, nx - 1, 2, tok // nt, hs), BF16),
         pltpu.VMEM((ns, nx - 1, 2, tok // nt, hs), BF16),
         pltpu.VMEM((ns, tok, hs), BF16),
         pltpu.VMEM((ns + 1, tok, width), BF16),
-        sem((4,)),
+        sem((5,)),
         sem((local_count,)),
         sem((local_count,)),
         sem((local_count,)),
         sem((2, ns - 1)),
-        sem((2, 2, ns, pieces)),
-        sem((2, ns, units)),
-        sem((2, ns, units, nx - 1)),
-        sem((2, ns, units, nx - 1)),
-        sem((2, ns, units, nx)),
+        sem((2, ns + 1, pieces)),
+        sem((2, 2, units)),
+        sem((2, 2, units, nx - 1)),
+        sem((2, 2, units, nx - 1)),
+        sem((2, 3, units, nx)),
         sem((2, ns + 1, width // cw)),
+        sem((2, 2, width // cw)),
+        sem(()),
     ]
     return pl.pallas_call(
         functools.partial(line_layer, dims),
         out_shape=jax.ShapeDtypeStruct((tok, width), BF16),
-        in_specs=[hbm] * 7,
-        out_specs=pl.BlockSpec(memory_space=pltpu.VMEM),
+        in_specs=[hbm] * 8,
+        out_specs=hbm,
         scratch_shapes=scratch,
         compiler_params=pltpu.CompilerParams(
             collective_id=0, has_side_effects=True, vmem_limit_bytes=65400 * 1024
         ),
         name="moe_line",
-    )(tokens, meta, expert_gate, expert_up, expert_down, shared_in, shared_down)
+    )(tokens, choices.T, affinity.T, expert_gate, expert_up, expert_down, shared_in, shared_down)
 
 
 def choose(tokens, choices, affinity, expert_gate, *rest):

time: 108 us -> 80.6 us (0.75)
  Pallas kernels: 103 us -> 78.2 us
  other arithmetic: 2.69 us -> 0 us
    pallas_call x1, Pallas kernels: 103 us -> 78.2 us  [line_local(): pl.pallas_call(functools.partial(line_layer, dims), out_shape=jax.ShapeDt...]
    transpose x2 -> x0, other arithmetic: 1.39 us -> none  [line_local(): meta = jnp.concatenate([choices.astype(F32).T, mix.T], axis=0)]
where the time goes in v1:
time: 80.6 us; the launch traced here: 80 us
  Pallas kernels  78.2 us (97%)
  local copies, waits for them, and re-layouts  1.82 us (2%)
    pallas_call x1, Pallas kernels, line_local(): pl.pallas_call(functools.partial(line_layer, dims), out_shape=jax.ShapeDt...  78.2 us
    unnamed x1, local copies, waits for them, and re-layouts  1.82 us

profile of v1, /device:TPU:0, one launch (start us, length us, event | category | flops | bytes accessed | tf_op | source)
XLA Modules:
  0.0 80.0 jit_solution(4969812861890064853)
XLA Ops:
  0.0 78.2 %moe_line.1 = bf16[128,1792]{1,0:T(8,128)(2,1)} custom-call(bf16[128,1792]{1,0:T(8,128)(2,1)} %tokens.1, s32[4,128]{1,0:T(4,128)} %bitcast.2, f32[4,128]{1,0:T(4,128)} %bitcast.3, bf16[1792,4096]{1,0:T(8,128)(2,1)} %gate_hbm.1, bf16[1792,4096]{1,0:T(8,128)(2,1)} %up_hbm.1, bf16[4096,1792]{1,0:T(8,128)(2,1)} %down_hbm.1, bf16[2,256,1792]{2,1,0:T(8,128)(2,1)} %sin_hbm.1, ...), custom_call_target="tpu_custom_call" | custom-call | tf_op jit(solution)/shard_map/moe_line/pallas_call | solution.py:907
  78.2 1.8 %copy.10 = bf16[128,1792]{1,0:T(8,128)(2,1)} copy(bf16[128,1792]{1,0:T(8,128)(2,1)} %moe_line.1) | data formatting | bytes 917504

commit v2 on v1

--- a/solution.py
+++ b/solution.py
@@ -490,15 +490,18 @@
                 p[g] = mm(block, sin_w[g], 1, 1).astype(BF16)
         else:
             e = u
-            lhs = rows[e]
+            first_row = e if e + 1 < local_count else max(e - 1, 0)
+            pair = min(2, local_count)
+            lhs = rows[first_row : first_row + pair].reshape(pair * cap, width)
+            keep = slice((e - first_row) * cap, (e - first_row + 1) * cap)
             if i == 0:
                 gate_loads[e].wait()
                 load_next(1)
-            p[0] = mm(lhs, gate_w[e]).astype(BF16)
+            p[0] = mm(lhs, gate_w[e])[keep].astype(BF16)
             if i == 0:
                 up_loads[e].wait()
                 load_next(1)
-            p[1] = mm(lhs, up_w[e]).astype(BF16)
+            p[1] = mm(lhs, up_w[e])[keep].astype(BF16)
         half = extent(u) // 2
         theirs = along(u, peer_c * half, half, (slice(None),))
         copy = remote(p.at[theirs], ci, core_sem, (i % 2, u), {"tensor": peer_t})
@@ -575,16 +578,15 @@
             return
         if i == 1:
             down_loads[u].wait()
-        count = len(span)
-        lhs = hid[u, pl.ds(span[0], count)].reshape(count * cap, piece)
-        result = mm(lhs, down_w[u]).astype(BF16)
-        for n, j in enumerate(span):
-            made[step_block(j), pl.ds(u * cap, cap), :] = result[n * cap : (n + 1) * cap]
+        lhs = hid[u, pl.ds(i - 1, 2)].reshape(2 * cap, piece)
+        result = mm(lhs, down_w[u])
+        for j in span:
+            n = j - i + 1
+            made[step_block(j), pl.ds(u * cap, cap), :] = result[n * cap : (n + 1) * cap].astype(BF16)
 
     parts = width // cw
 
-    def contribution(b, k):
-        span = pl.ds(k * cw, cw)
+    def contribution(b, span):
         return mm(comb[b], made[b, :, span], 0, 0) + mm(s_hid[b], sdown_w[:, span])
 
     half_rows = tok // 2
@@ -610,14 +612,19 @@
     def originate(r, span):
         @pl.when(zeta == 0)
         def _():
+            end = r + 1 == ns
+            wide = pl.ds(span[0] * cw, len(span) * cw)
+            if not end:
+                x_all[phys(r), :, wide] = contribution(phys(r), wide).astype(BF16)
             for k in span:
-                x_all[phys(r), :, pl.ds(k * cw, cw)] = contribution(phys(r), k).astype(BF16)
-                end = r + 1 == ns
+                if end:
+                    one = pl.ds(k * cw, cw)
+                    x_all[phys(r), :, one] = contribution(phys(r), one).astype(BF16)
                 for h in range(len(spans(end))):
                     rs_copy(True, r, k, h, end, above).start()
 
     def relay(upward, b, k):
-        value = contribution(phys(b), k)
+        value = contribution(phys(b), pl.ds(k * cw, cw))
         end = b + 1 == ns if upward else b == 0
         for h, side in enumerate(spans(end)):
             total = value[side.start : side.start + side.size] + arrived(upward, b, k, h, end)
@@ -646,6 +653,7 @@
         pl.when(zeta == 0)(functools.partial(arrive, i, k))
 
     last = units - 1
+    late = []
     for i in range(ns):
         if i == 1:
             outer(1, 0)
@@ -656,71 +664,58 @@
             outer(i, 0)
             outer(i, 1)
         dispatch(step_block(i))
+        relays = list(range(units)) if i else []
         for u in range(units):
             run("A", i, u)
             if u > 0:
                 run("B", i, u - 1)
-            if i == 0:
-                if u >= 2:
-                    run("C", i, u - 2)
-                if u == 2:
-                    inner(1, 0)
-            else:
-                if u == 0:
-                    inner(i + 1, 1)
-                if i < 3 and u < 2:
-                    for v in range(-(-len(late) // (2 - u))):
-                        run("C", i - 1, late.pop(0))
-                if i > 2 and u == 0:
-                    for v in range(units - 2):
-                        run("D", i - 1, v)
-                    relays = [units - 2, last]
-                elif u == 1 and i < 3:
-                    run("D", i - 1, 0)
-                    run("D", i - 1, 1)
-                    relays = list(range(2, units))
-                elif u >= 3 or (i > 2 and u > 0):
-                    for v in range(-(-len(relays) // (units - u)) if i < 3 else 1):
-                        if relays:
-                            run("D", i - 1, relays.pop(0))
-                if u >= 3:
-                    run("C", i, u - 3)
+            if i == 0 and u == 2:
+                inner(1, 0)
+            if i > 0 and u == 0:
+                inner(i + 1, 1)
+            if u < 2 and late:
+                for v in range(-(-len(late) // (2 - u))):
+                    run("C", i - 1, late.pop(0))
+            if relays and (i > 2 or u >= 3):
+                share = units - 2 if i > 2 and u == 0 else 1 if i > 2 else -(-len(relays) // (units - u))
+                for v in range(min(share, len(relays))):
+                    run("D", i - 1, relays.pop(0))
+        for v in relays:
+            run("D", i - 1, v)
+        run("C", i, 0)
+        rest = list(range(1, units))
         if i > 0:
             inner(i + 2, 0)
-        if i == 0:
+        else:
             load_next(len(queue))
-            run("B", 0, last)
-            late = [units - 2, last]
+        if i < 2:
+            run("B", i, last)
+            late = rest
             continue
-        rest = list(range(units - 3, last))
-        if i == 1:
-            run("B", i, last)
-            late = rest + [last]
-            if i + 1 < ns:
-                continue
-            rest = late
-        else:
-            for u in range(units):
-                run("E", i - 1, u)
-                if u == 0:
-                    run("B", i, last)
-                elif rest and u < last:
-                    run("C", i, rest.pop(0))
-            originate(i - 1, range(early if i + 1 == ns else parts))
-            rest.append(last)
-        if i + 1 < ns:
-            for u in rest:
-                run("C", i, u)
-    for u in rest:
-        run("C", ns - 1, u)
-    for u in range(units):
-        if u == last:
-            run("E", ns - 1, u - 2)
+        final = i + 1 == ns
+        relays = list(range(units))
+        for u in range(units):
+            run("E", i - 1, u)
+            if u == 0:
+                run("B", i, last)
+            if u < 2 or u == last - 1:
+                run("C", i, rest.pop(0))
+        if final:
+            run("D", i, relays.pop(0))
+            run("D", i, relays.pop(0))
+        originate(i - 1, range(early if final else parts))
+        for u in rest:
+            run("C", i, u)
+    done = 0
+    for u in relays:
         run("D", ns - 1, u)
-        if 2 <= u < last:
-            run("E", ns - 1, u - 2)
-    run("E", ns - 1, last - 1)
-    run("E", ns - 1, last)
+        while done < u:
+            run("E", ns - 1, done)
+            done += 1
+            if done == u - 1 and u > 2:
+                break
+    for u in range(done, units):
+        run("E", ns - 1, u)
     originate(ns - 1, range(parts))
     if ns > 2:
         originate(ns - 2, range(early, parts))
@@ -757,7 +752,7 @@
     def finish(inside):
         for k in range(parts):
             span = pl.ds(k * cw, cw)
-            value = contribution(z, k)
+            value = contribution(z, span)
             for h, side in enumerate(spans(not inside)):
                 total = value[side.start : side.start + side.size] + arrived(False, zeta, k, h, not inside)
                 if inside:
@@ -921,7 +916,7 @@
     tok = tokens.shape[0]
     ns, nt = lax.axis_size("expert"), lax.axis_size("tensor")
     piece = min(FFE, expert_gate.shape[1])
-    fits = ns % 2 == 0 and piece % (128 * nt) == 0 and tok % (16 * nt) == 0 and expert_gate.shape[1] % piece == 0
+    fits = ns % 2 == 0 and ns > 2 and piece % (128 * nt) == 0 and tok % (16 * nt) == 0 and expert_gate.shape[1] % piece == 0
     which = line_local if fits else local
     return which(tokens, choices, affinity, expert_gate, *rest)
 

time: 80.6 us -> 77.7 us (0.964)
  Pallas kernels: 78.2 us -> 75.7 us
    pallas_call x1, Pallas kernels: 78.2 us -> 75.7 us  [line_local(): pl.pallas_call(functools.partial(line_layer, dims), out_shape=jax.ShapeDt...]
where the time goes in v2:
time: 77.7 us; the launch traced here: 77.5 us
  Pallas kernels  75.7 us (97%)
  local copies, waits for them, and re-layouts  1.82 us (2%)
    pallas_call x1, Pallas kernels, line_local(): pl.pallas_call(functools.partial(line_layer, dims), out_shape=jax.ShapeDt...  75.7 us
    unnamed x1, local copies, waits for them, and re-layouts  1.82 us

profile of v2, /device:TPU:0, one launch (start us, length us, event | category | flops | bytes accessed | tf_op | source)
XLA Modules:
  0.0 77.5 jit_solution(4554863444421188635)
XLA Ops:
  0.0 75.7 %moe_line.1 = bf16[128,1792]{1,0:T(8,128)(2,1)} custom-call(bf16[128,1792]{1,0:T(8,128)(2,1)} %tokens.1, s32[4,128]{1,0:T(4,128)} %bitcast.2, f32[4,128]{1,0:T(4,128)} %bitcast.3, bf16[1792,4096]{1,0:T(8,128)(2,1)} %gate_hbm.1, bf16[1792,4096]{1,0:T(8,128)(2,1)} %up_hbm.1, bf16[4096,1792]{1,0:T(8,128)(2,1)} %down_hbm.1, bf16[2,256,1792]{2,1,0:T(8,128)(2,1)} %sin_hbm.1, ...), custom_call_target="tpu_custom_call" | custom-call | tf_op jit(solution)/shard_map/moe_line/pallas_call | solution.py:902
  75.7 1.8 %copy.10 = bf16[128,1792]{1,0:T(8,128)(2,1)} copy(bf16[128,1792]{1,0:T(8,128)(2,1)} %moe_line.1) | data formatting | bytes 917504
